TPU v7x, 128 devices: a whole 4x4x4 slice. The times are simulated.
128 devices in a mesh: fsdp: 16 (over x_lo, y, core), expert: 8 (over x_hi, z).
Axes of the slice: x: 4 (x_hi: 2, x_lo: 2; x = x_hi * 2 + x_lo), y: 4, z: 4, core: 2. Of those that a mesh axis runs over, the one named last changes fastest.
Arguments:
- pool: bfloat16 [256, 128, 4096], P('fsdp', None, 'expert'), may hold values from -6 to 6
- picks: int32 [16, 8], P('fsdp'), may hold values from 0 to 15, as said below
- lengths: int32 [256], P('fsdp'), may hold values from 1 to 128
- routes: int32 [16384, 2], P(('fsdp', 'expert')), may hold values from 0 to 7, all different within a row; in each aligned block of 128 rows (0 to 127, 128 to 255, ...) at most 64 rows name the same one
- route_gap: float32 [16384], P(('fsdp', 'expert')), may hold values from -8 to 8
- gate_weight: bfloat16 [8, 14336, 4096], P('expert', 'fsdp'), may hold values from -0.09375 to 0.09375
- down_weight: bfloat16 [8, 14336, 4096], P('expert', 'fsdp'), may hold values from -0.046875 to 0.046875
Outputs:
- moe_out: bfloat16 [16384, 4096], P(('fsdp', 'expert'))
Inputs may be any that keep to these rules, and one draw needn't show every extreme that they name: `picks`: each row holds 8 different candidate numbers. `routes`: the two experts of a token differ; among the 128 tokens of one window no expert is named by more than 64 tokens.
All inputs are finite; a program needn't handle non-finite values.
Results may differ from a plain program's by a relative error of at most 0.019.
Values may be sent and summed in bfloat16 or wider, within the bound.
A program may use at most 128 MiB of HBM per device.

v0:
```python
import jax
import jax.numpy as jnp
from jax import lax
from jax.sharding import PartitionSpec as P

EXPERTS = 8
TOP = 2
CAP = 14


def sent_to_all(value, axis):
    length = lax.axis_size(axis)
    return lax.all_to_all(
        jnp.broadcast_to(value[None], (length, *value.shape)), axis, 0, 0, tiled=True
    )


def laid_out(tiles, dim):
    shape = list(tiles.shape[1:])
    shape[dim] *= tiles.shape[0]
    return jnp.moveaxis(tiles, 0, dim).reshape(shape)


def collect(value, axis, dim):
    tiles = sent_to_all(value, axis)
    return laid_out(tiles, dim)


def slot_targets(block_routes, length):
    row_count = block_routes.shape[0]
    is_live = jnp.arange(row_count, dtype=jnp.int32) < length
    expert_ids = jnp.concatenate([block_routes[:, 0], block_routes[:, 1]])
    live_both = jnp.concatenate([is_live, is_live])
    expert_hits = (
        (expert_ids[:, None] == jnp.arange(EXPERTS, dtype=jnp.int32)[None, :]) & live_both[:, None]
    ).astype(jnp.int32)
    earlier = jnp.cumsum(expert_hits, axis=0) - expert_hits
    slot_rank = jnp.sum(earlier * expert_hits, axis=1)
    is_kept = live_both & (slot_rank < CAP)
    return jnp.where(is_kept, expert_ids * CAP + slot_rank, -1)


def dispatch_table(targets):
    row_count = targets.shape[0] // 2
    slot_ids = jnp.arange(EXPERTS * CAP, dtype=jnp.int32)[:, None]
    return (
        (slot_ids == targets[None, :row_count]) | (slot_ids == targets[None, row_count:])
    ).astype(jnp.bfloat16)


def combine_table(targets, gap_row):
    row_count = targets.shape[0] // 2
    slot_ids = jnp.arange(EXPERTS * CAP, dtype=jnp.int32)[None, :]
    weight_first = jax.nn.sigmoid(gap_row)[:, None]
    weight_second = jax.nn.sigmoid(-gap_row)[:, None]
    first_hit = (targets[:row_count, None] == slot_ids).astype(jnp.float32)
    second_hit = (targets[row_count:, None] == slot_ids).astype(jnp.float32)
    return first_hit * weight_first + second_hit * weight_second


def local(pool, picks, lengths, routes, route_gap, gate_weight, down_weight):
    expert_count = lax.axis_size("expert")
    expert_local = gate_weight.shape[0]
    window_rows = pool.shape[1]
    model_width = gate_weight.shape[2]
    my_column = lax.axis_index("expert")
    chosen = picks[0]
    selected = jnp.take(pool, chosen, axis=0)
    chosen_len = jnp.take(lengths, chosen)
    column_routes = collect(routes, "expert", 0)
    all_targets = jax.vmap(slot_targets)(
        column_routes.reshape(expert_count, window_rows, TOP), chosen_len
    )
    tables = jax.vmap(dispatch_table)(all_targets)
    outgoing = jnp.einsum(
        "bsp,bpd->bsd", tables, selected, preferred_element_type=jnp.float32
    ).astype(jnp.bfloat16)
    outgoing = outgoing.reshape(expert_count, expert_count, expert_local, CAP, selected.shape[2])
    arrived = lax.all_to_all(outgoing, "expert", split_axis=1, concat_axis=4, tiled=True)
    arrived = arrived.reshape(expert_count, expert_local, CAP, model_width)
    my_targets = lax.dynamic_index_in_dim(all_targets, my_column, 0, keepdims=False)
    gate_act = jnp.einsum(
        "fbecd,ehd->fbech",
        lax.all_gather(arrived[None], "fsdp", axis=0, tiled=True),
        gate_weight,
        preferred_element_type=jnp.float32,
    )
    hidden = jax.nn.silu(gate_act).astype(jnp.bfloat16)
    dev_rows = expert_count * expert_local * CAP
    partial_value = jnp.einsum(
        "fbech,ehd->fbecd", hidden, down_weight, preferred_element_type=jnp.float32
    )
    summed = lax.psum_scatter(
        partial_value.reshape(dev_rows * lax.axis_size("fsdp"), model_width).astype(jnp.bfloat16),
        "fsdp",
        scatter_dimension=0,
        tiled=True,
    )
    expert_out = summed.reshape(expert_count, expert_local, CAP, model_width)
    returned = lax.all_to_all(expert_out, "expert", split_axis=0, concat_axis=1, tiled=True)
    flat_out = returned.reshape(EXPERTS * CAP, model_width).astype(jnp.float32)
    combine = combine_table(my_targets, route_gap)
    mixed = jnp.dot(combine, flat_out, preferred_element_type=jnp.float32)
    return mixed.astype(jnp.bfloat16)


def solution(mesh):
    placed = (
        P("fsdp", None, "expert"),
        P("fsdp", None),
        P("fsdp"),
        P(("fsdp", "expert"), None),
        P(("fsdp", "expert")),
        P("expert", "fsdp", None),
        P("expert", "fsdp", None),
    )
    return jax.shard_map(
        local, mesh=mesh, in_specs=placed, out_specs=P(("fsdp", "expert"), None), check_vma=False
    )
```

profile of v0, /device:TPU:0, one launch (start us, length us, event | category | flops | bytes accessed | tf_op | source)
XLA Modules:
  0.0 329.3 jit_solution(543143658603108437)
XLA Ops:
  6.5 0.0 copy-start
  6.5 1.4 broadcast_in_dim.17
  8.0 7.9 %all-to-all-start = ((s32[8,128,2]{1,2,0:T(2,128)}), s32[8,128,2]{1,2,0:T(2,128)S(1)}, u32[]{:S(2)}, u32[]{:S(2)}) async-start(s32[8,128,2]{1,2,0:T(2,128)} %broadcast_in_dim.17), calls=%async_computation | async-start | bytes 16384 | tf_op jit(solution)/shard_map/all_to_all | solution.py:13
  15.9 0.0 all-gather.2.cloned.1.call-start
  15.9 0.7 fusion.35
  16.6 1.3 gather_fusion
  17.9 0.7 broadcast_select_fusion
  18.5 0.1 iota_compare_fusion.10
  18.6 0.1 iota_compare_fusion.9
  18.7 0.0 copy-done
  18.7 0.6 gather_fusion.1
  19.3 4.2 %all-to-all-done = s32[8,128,2]{1,2,0:T(2,128)S(1)} async-done(((s32[8,128,2]{1,2,0:T(2,128)}), s32[8,128,2]{1,2,0:T(2,128)S(1)}, u32[]{:S(2)}, u32[]{:S(2)}) %all-to-all-start) | async-done | bytes 8224 | tf_op jit(solution)/shard_map/all_to_all | solution.py:13
  23.6 4.5 %reduce-window.6 = s32[8,8,2,128]{3,1,2,0:T(8,128)S(1)} reduce-window(s32[8,8,2,128]{3,1,2,0:T(8,128)S(1)} %fusion.27, s32[]{:T(128)} %constant.36.clone.1), window={size=1x1x1x128 pad=0_0x0_0x0_0x127_0}, to_apply=%region_0.1 | reduce-window | flops 2080768 | bytes 131076 | tf_op jit(solution)/shard_map/reduce-window
  28.1 0.1 slice.40
  28.2 0.2 copy.28
  28.4 0.1 fusion.33
  28.5 0.1 fusion.21
  28.6 0.5 convolution_convert_fusion.1
  29.1 0.5 copy.30
  29.6 18.0 %all_to_all.29 = bf16[8,8,1,14,512]{4,0,3,2,1:T(8,128)(2,1)S(1)} all-to-all(bf16[8,8,1,14,512]{4,0,3,2,1:T(8,128)(2,1)S(1)} %bitcast.91), channel_id=1, replica_groups=mesh['fsdp'=16,'expert'=8] {'expert'}, dimensions={1} | all-to-all | bytes 1835008 | tf_op jit(solution)/shard_map/all_to_all | solution.py:79
  47.6 0.5 copy.32
  48.1 1.3 broadcast_in_dim_reshape.3
  49.5 0.0 all-gather.2.cloned.1.call-update
  49.5 0.2 reduce-scatter.2.cloned.1.call-start
  49.7 78.9 %all-gather.2.cloned.1.call-done = bf16[16,8,1,14,4096]{4,1,3,2,0:T(8,128)(2,1)} async-done(((bf16[1,8,1,14,4096]{4,1,3,2,0:T(8,128)(2,1)}), bf16[16,8,1,14,4096]{4,1,3,2,0:T(8,128)(2,1)}) %all-gather.2.cloned.1.call-update) | async-done | bytes 14680080 | tf_op jit(solution)/shard_map/all_gather | solution.py:84
  128.6 20.7 %fusion.7 = bf16[16,8,1,14,896]{4,1,3,0,2:T(8,128)(2,1)S(1)} fusion(bf16[1,896,4096]{2,1,0:T(8,128)(2,1)} %param.12, bf16[16,8,1,14,4096]{4,1,3,2,0:T(8,128)(2,1)} %all-gather.2.cloned.1.call-done), kind=kOutput, calls=%fused_computation.12 | convolution fusion | flops 13161365504 | bytes 25231360 | tf_op jit(solution)/shard_map/fbecd,ehd->fbech/dot_general | solution.py:82
  149.4 20.9 %convert_bitcast_fusion = bf16[16,8,1,14,4096]{4,1,3,0,2:T(8,128)(2,1)} fusion(bf16[1,896,4096]{2,1,0:T(8,128)(2,1)} %param.13, bf16[16,8,1,14,896]{4,1,3,0,2:T(8,128)(2,1)S(1)} %fusion.7), kind=kOutput, calls=%fused_computation.4 | convolution fusion | flops 13160677376 | bytes 25231360 | tf_op jit(solution)/shard_map/fbech,ehd->fbecd/dot_general | solution.py:90
  170.3 17.5 %copy.33 = bf16[16,8,1,14,4096]{4,3,1,0,2:T(8,128)(2,1)} copy(bf16[16,8,1,14,4096]{4,1,3,0,2:T(8,128)(2,1)} %convert_bitcast_fusion) | data formatting | bytes 29360128 | tf_op jit(solution)/shard_map/convert_element_type | solution.py:94
  187.7 18.0 %convert_element_type.43 = bf16[1792,4096]{1,0:T(8,128)(2,1)} reshape(bf16[16,8,1,14,4096]{4,3,1,0,2:T(8,128)(2,1)} %copy.33) | data formatting | bytes 29360128 | tf_op jit(solution)/shard_map/convert_element_type | solution.py:94
  205.8 0.0 copy-start.2
  205.8 0.0 reduce-scatter.2.cloned.1.call-update
  205.8 0.0 copy-start.1
  205.8 90.1 %reduce-scatter.2.cloned.1.call-done = bf16[112,4096]{1,0:T(8,128)(2,1)} async-done(((bf16[1792,4096]{1,0:T(8,128)(2,1)}), bf16[112,4096]{1,0:T(8,128)(2,1)}) %reduce-scatter.2.cloned.1.call-update) | async-done | bytes 917520 | tf_op jit(solution)/shard_map/reduce_scatter | solution.py:93
  295.9 2.4 reshape.152
  298.3 6.8 %all-to-all-start.2 = ((bf16[8,1,14,4096]{3,2,1,0:T(8,128)(2,1)}), bf16[8,1,14,4096]{3,2,1,0:T(8,128)(2,1)S(1)}, u32[]{:S(2)}, u32[]{:S(2)}) async-start(bf16[8,1,14,4096]{3,2,1,0:T(8,128)(2,1)} %bitcast.90), calls=%async_computation.3 | async-start | bytes 2097152 | tf_op jit(solution)/shard_map/all_to_all | solution.py:100
  305.1 0.0 copy-done.2
  305.1 0.1 dynamic-slice_bitcast_fusion.1
  305.2 13.4 %all-to-all-done.2 = bf16[8,1,14,4096]{3,2,1,0:T(8,128)(2,1)S(1)} async-done(((bf16[8,1,14,4096]{3,2,1,0:T(8,128)(2,1)}), bf16[8,1,14,4096]{3,2,1,0:T(8,128)(2,1)S(1)}, u32[]{:S(2)}, u32[]{:S(2)}) %all-to-all-start.2) | async-done | bytes 917536 | tf_op jit(solution)/shard_map/all_to_all | solution.py:100
  318.6 1.2 reshape.153
  319.8 2.7 convolution_convert_fusion
  322.4 0.0 copy-done.1
  (13 shorter events, 0.1 us)
Async XLA Ops:
  6.5 12.2 %copy-start = (bf16[16,128,512]{2,1,0:T(8,128)(2,1)S(1)}, bf16[16,128,512]{2,1,0:T(8,128)(2,1)}, u32[]{:S(2)}) copy-start(bf16[16,128,512]{2,1,0:T(8,128)(2,1)} %param.7) | copy-start | bytes 6291460
  8.0 15.6 %all-to-all-start = ((s32[8,128,2]{1,2,0:T(2,128)}), s32[8,128,2]{1,2,0:T(2,128)S(1)}, u32[]{:S(2)}, u32[]{:S(2)}) async-start(s32[8,128,2]{1,2,0:T(2,128)} %broadcast_in_dim.17), calls=%async_computation | async-start | bytes 16384 | tf_op jit(solution)/shard_map/all_to_all | solution.py:13
  15.9 112.8 %all-gather.2.cloned.1.call-start = ((), (), s32[]{:S(2)}) async-start(), calls=%async_computation.4 | async-start | bytes 15597568 | tf_op jit(solution)/shard_map/all_gather | solution.py:84
  49.5 246.4 %reduce-scatter.2.cloned.1.call-start = ((), (), s32[]{:S(2)}) async-start(), calls=%async_computation.5 | async-start | bytes 15597568 | tf_op jit(solution)/shard_map/reduce_scatter | solution.py:93
  205.8 99.3 %copy-start.2 = (f32[128]{0:T(128)S(1)}, f32[128]{0:T(128)}, u32[]{:S(2)}) copy-start(f32[128]{0:T(128)} %param.11) | copy-start | bytes 1540
  205.8 116.7 %copy-start.1 = (bf16[16,128,512]{2,1,0:T(8,128)(2,1)S(1)}, bf16[16,128,512]{2,1,0:T(8,128)(2,1)}, u32[]{:S(2)}) copy-start(bf16[16,128,512]{2,1,0:T(8,128)(2,1)} %param.7) | copy-start | bytes 6291460
  298.3 20.3 %all-to-all-start.2 = ((bf16[8,1,14,4096]{3,2,1,0:T(8,128)(2,1)}), bf16[8,1,14,4096]{3,2,1,0:T(8,128)(2,1)S(1)}, u32[]{:S(2)}, u32[]{:S(2)}) async-start(bf16[8,1,14,4096]{3,2,1,0:T(8,128)(2,1)} %bitcast.90), calls=%async_computation.3 | async-start | bytes 2097152 | tf_op jit(solution)/shard_map/all_to_all | solution.py:100
Sparse Core Ops, SparseCore 0:
  49.6 78.9 all-gather.1
  205.9 89.9 reduce-scatter.1
where the time goes:
time: 330 us; the launch traced here: 329 us
  waiting for transfers between devices  187 us (57%)
  local copies, waits for them, and re-layouts  45.2 us (14%)
  matrix products  44.8 us (14%)
  blocking collectives  18 us (5%)
  starting transfers between devices  14.9 us (5%)
  between operations  13.6 us (4%)
  other arithmetic  6.23 us (2%)
    reduce_scatter x1, waiting for transfers between devices, local(): lax.psum_scatter(partial_value.reshape(dev_rows * lax.axis_size('fsdp'),...  90.1 us
    all_gather x1, waiting for transfers between devices, local(): lax.all_gather(arrived[None], 'fsdp', axis=0, tiled=True)  78.9 us
    convert_element_type x2, local copies, waits for them, and re-layouts, local(): partial_value.reshape(dev_rows * lax.axis_size('fsdp'), model_width)  35.5 us
    dot_general x1, matrix products, local(): jnp.einsum('fbech,ehd->fbecd', hidden, down_weight, preferred_element_typ...  20.9 us
    dot_general x1, matrix products, local(): jnp.einsum('fbecd,ehd->fbech', lax.all_gather(arrived[None], 'fsdp', axis...  20.7 us
    all_to_all x1, blocking collectives, local(): lax.all_to_all(outgoing, 'expert', split_axis=1, concat_axis=4, tiled=True)  18 us
    all_to_all x1, waiting for transfers between devices, local(): lax.all_to_all(expert_out, 'expert', split_axis=0, concat_axis=1, tiled=T...  13.4 us
    all_to_all x1, starting transfers between devices, sent_to_all(): lax.all_to_all(jnp.broadcast_to(value[None], (length, *value.shape)), axi...  7.89 us
  transfers between devices with their start and end apart: 4, of which 4 were waited for; matrix products, arithmetic and copies ran while one was open for 1% of the time, Pallas kernels for 0%

commit v1 on v0

--- a/solution.py
+++ b/solution.py
@@ -81,7 +81,9 @@
     my_targets = lax.dynamic_index_in_dim(all_targets, my_column, 0, keepdims=False)
     gate_act = jnp.einsum(
         "fbecd,ehd->fbech",
-        lax.all_gather(arrived[None], "fsdp", axis=0, tiled=True),
+        jnp.concatenate(
+            lax.all_to_all(jnp.stack([arrived[None]] * lax.axis_size("fsdp")), "fsdp", 0, 0), axis=0
+        ),
         gate_weight,
         preferred_element_type=jnp.float32,
     )

time: 330 us -> 420 us (1.27)
  blocking collectives: 18 us -> 187 us
  waiting for transfers between devices: 187 us -> 102 us
  local copies, waits for them, and re-layouts: 45.2 us -> 51.3 us
    all_to_all x0 -> x1, blocking collectives: none -> 169 us  [local(): lax.all_to_all(jnp.stack([arrived[None]] * lax.axis_size('fsdp')), 'fsdp'...]
    all_gather x1 -> x0, waiting for transfers between devices: 78.9 us -> none  [local(): lax.all_gather(arrived[None], 'fsdp', axis=0, tiled=True)]
    reduce_scatter x1, waiting for transfers between devices: 90.1 us -> 83.9 us  [local(): lax.psum_scatter(partial_value.reshape(dev_rows * lax.axis_size('fsdp'),...]
    another operation x3 -> x4, local copies, waits for them, and re-layouts: 1.35 us -> 7.44 us  [the longest x2 7.43 us: local(): jnp.stack([arrived[None]] * lax.axis_size('fsdp'))]
  transfers between devices with their start and end apart: 4 -> 3, of which waited for: 4 -> 3; matrix products, arithmetic and copies ran while one was open for 1% -> 1% of each run, Pallas kernels for 0% -> 0%
where the time goes in v1:
time: 420 us; the launch traced here: 419 us
  blocking collectives  187 us (45%)
  waiting for transfers between devices  102 us (24%)
  local copies, waits for them, and re-layouts  51.3 us (12%)
  matrix products  44.8 us (11%)
  starting transfers between devices  15 us (4%)
  between operations  13.6 us (3%)
  other arithmetic  6.23 us (1%)
    all_to_all x1, blocking collectives, local(): lax.all_to_all(jnp.stack([arrived[None]] * lax.axis_size('fsdp')), 'fsdp'...  169 us
    reduce_scatter x1, waiting for transfers between devices, local(): lax.psum_scatter(partial_value.reshape(dev_rows * lax.axis_size('fsdp'),...  83.9 us
    convert_element_type x2, local copies, waits for them, and re-layouts, local(): partial_value.reshape(dev_rows * lax.axis_size('fsdp'), model_width)  35.5 us
    dot_general x1, matrix products, local(): jnp.einsum('fbecd,ehd->fbech', jnp.concatenate(lax.all_to_all(jnp.stack([...  21.8 us
    dot_general x1, matrix products, local(): jnp.einsum('fbech,ehd->fbecd', hidden, down_weight, preferred_element_typ...  19.8 us
    all_to_all x1, blocking collectives, local(): lax.all_to_all(outgoing, 'expert', split_axis=1, concat_axis=4, tiled=True)  18 us
    all_to_all x1, waiting for transfers between devices, local(): lax.all_to_all(expert_out, 'expert', split_axis=0, concat_axis=1, tiled=T...  13.4 us
  transfers between devices with their start and end apart: 3, of which 3 were waited for; matrix products, arithmetic and copies ran while one was open for 1% of the time, Pallas kernels for 0%

profile of v1, /device:TPU:0, one launch (start us, length us, event | category | flops | bytes accessed | tf_op | source)
XLA Modules:
  0.0 419.0 jit_solution(9792713057598010121)
XLA Ops:
  6.5 0.0 copy-start
  6.5 1.4 broadcast_in_dim.17
  8.0 7.9 %all-to-all-start = ((s32[8,128,2]{1,2,0:T(2,128)}), s32[8,128,2]{1,2,0:T(2,128)S(1)}, u32[]{:S(2)}, u32[]{:S(2)}) async-start(s32[8,128,2]{1,2,0:T(2,128)} %broadcast_in_dim.17), calls=%async_computation | async-start | bytes 16384 | tf_op jit(solution)/shard_map/all_to_all | solution.py:13
  15.9 0.0 reduce-scatter.2.cloned.1.call-start
  15.9 0.7 fusion.35
  16.6 1.3 gather_fusion
  17.9 0.7 broadcast_select_fusion
  18.5 0.1 iota_compare_fusion.10
  18.6 0.1 iota_compare_fusion.9
  18.7 0.0 copy-done
  18.7 0.6 gather_fusion.1
  19.3 4.2 %all-to-all-done = s32[8,128,2]{1,2,0:T(2,128)S(1)} async-done(((s32[8,128,2]{1,2,0:T(2,128)}), s32[8,128,2]{1,2,0:T(2,128)S(1)}, u32[]{:S(2)}, u32[]{:S(2)}) %all-to-all-start) | async-done | bytes 8224 | tf_op jit(solution)/shard_map/all_to_all | solution.py:13
  23.6 4.5 %reduce-window.6 = s32[8,8,2,128]{3,1,2,0:T(8,128)S(1)} reduce-window(s32[8,8,2,128]{3,1,2,0:T(8,128)S(1)} %fusion.27, s32[]{:T(128)} %constant.36.clone.1), window={size=1x1x1x128 pad=0_0x0_0x0_0x127_0}, to_apply=%region_0.1 | reduce-window | flops 2080768 | bytes 131076 | tf_op jit(solution)/shard_map/reduce-window
  28.1 0.1 slice.40
  28.2 0.2 copy.19
  28.4 0.1 fusion.33
  28.5 0.1 fusion.21
  28.6 0.5 convolution_convert_fusion.1
  29.1 0.5 copy.21
  29.6 18.0 %all_to_all.34 = bf16[8,8,1,14,512]{4,0,3,2,1:T(8,128)(2,1)S(1)} all-to-all(bf16[8,8,1,14,512]{4,0,3,2,1:T(8,128)(2,1)S(1)} %bitcast.91), channel_id=1, replica_groups=mesh['fsdp'=16,'expert'=8] {'expert'}, dimensions={1} | all-to-all | bytes 1835008 | tf_op jit(solution)/shard_map/all_to_all | solution.py:79
  47.6 0.5 copy.23
  48.1 0.4 stack_broadcast_in_dim_reshape.2
  48.5 7.0 %stack.3 = bf16[16,1,8,1,14,4096]{5,2,4,3,1,0:T(8,128)(2,1)} broadcast(bf16[8,14,4096]{2,0,1:T(8,128)(2,1)S(1)} %stack_broadcast_in_dim_reshape.2), dimensions={2,4,5} | broadcast | bytes 15597568 | tf_op jit(solution)/shard_map/stack | solution.py:85
  55.6 0.0 slice-start
  55.6 168.6 %all_to_all.35 = bf16[16,1,8,1,14,4096]{5,2,4,3,1,0:T(8,128)(2,1)} all-to-all(bf16[16,1,8,1,14,4096]{5,2,4,3,1,0:T(8,128)(2,1)} %stack.3), channel_id=1, replica_groups=mesh['fsdp'=16,'expert'=8] {'fsdp'}, dimensions={0} | all-to-all | bytes 29360128 | tf_op jit(solution)/shard_map/all_to_all | solution.py:85
  224.2 0.0 slice-start.1
  224.2 21.8 %fusion.7 = bf16[16,8,1,14,896]{4,1,3,0,2:T(8,128)(2,1)} fusion(bf16[1,896,4096]{2,1,0:T(8,128)(2,1)} %param.12, bf16[16,1,8,1,14,4096]{5,2,4,3,1,0:T(8,128)(2,1)} %all_to_all.35), kind=kOutput, calls=%fused_computation.12 | convolution fusion | flops 13161365504 | bytes 25231360 | tf_op jit(solution)/shard_map/fbecd,ehd->fbech/dot_general | solution.py:82
  245.9 0.0 slice-done
  245.9 0.0 slice-done.1
  246.0 19.8 %convert_bitcast_fusion = bf16[16,8,1,14,4096]{4,1,3,0,2:T(8,128)(2,1)} fusion(bf16[1,896,4096]{2,1,0:T(8,128)(2,1)S(1)} %bitcast.100, bf16[16,8,1,14,896]{4,1,3,0,2:T(8,128)(2,1)} %fusion.7), kind=kOutput, calls=%fused_computation.4 | convolution fusion | flops 13160677376 | bytes 25231360 | tf_op jit(solution)/shard_map/fbech,ehd->fbecd/dot_general | solution.py:92
  265.8 17.5 %copy.24 = bf16[16,8,1,14,4096]{4,3,1,0,2:T(8,128)(2,1)} copy(bf16[16,8,1,14,4096]{4,1,3,0,2:T(8,128)(2,1)} %convert_bitcast_fusion) | data formatting | bytes 29360128 | tf_op jit(solution)/shard_map/convert_element_type | solution.py:96
  283.3 18.0 %convert_element_type.43 = bf16[1792,4096]{1,0:T(8,128)(2,1)} reshape(bf16[16,8,1,14,4096]{4,3,1,0,2:T(8,128)(2,1)} %copy.24) | data formatting | bytes 29360128 | tf_op jit(solution)/shard_map/convert_element_type | solution.py:96
  301.3 0.0 copy-start.2
  301.3 0.0 reduce-scatter.2.cloned.1.call-update
  301.3 0.0 copy-start.1
  301.3 83.9 %reduce-scatter.2.cloned.1.call-done = bf16[112,4096]{1,0:T(8,128)(2,1)} async-done(((bf16[1792,4096]{1,0:T(8,128)(2,1)}), bf16[112,4096]{1,0:T(8,128)(2,1)}) %reduce-scatter.2.cloned.1.call-update) | async-done | bytes 917520 | tf_op jit(solution)/shard_map/reduce_scatter | solution.py:95
  385.3 2.4 reshape.158
  387.7 7.1 %all-to-all-start.3 = ((bf16[8,1,14,4096]{3,2,1,0:T(8,128)(2,1)}), bf16[8,1,14,4096]{3,2,1,0:T(8,128)(2,1)S(1)}, u32[]{:S(2)}, u32[]{:S(2)}) async-start(bf16[8,1,14,4096]{3,2,1,0:T(8,128)(2,1)} %bitcast.90), calls=%async_computation.4 | async-start | bytes 2097152 | tf_op jit(solution)/shard_map/all_to_all | solution.py:102
  394.8 0.0 copy-done.2
  394.8 0.1 dynamic-slice_bitcast_fusion.1
  394.9 13.4 %all-to-all-done.3 = bf16[8,1,14,4096]{3,2,1,0:T(8,128)(2,1)S(1)} async-done(((bf16[8,1,14,4096]{3,2,1,0:T(8,128)(2,1)}), bf16[8,1,14,4096]{3,2,1,0:T(8,128)(2,1)S(1)}, u32[]{:S(2)}, u32[]{:S(2)}) %all-to-all-start.3) | async-done | bytes 917536 | tf_op jit(solution)/shard_map/all_to_all | solution.py:102
  408.3 1.2 reshape.159
  409.5 2.7 convolution_convert_fusion
  412.1 0.0 copy-done.1
  (14 shorter events, 0.1 us)
Async XLA Ops:
  6.5 12.2 %copy-start = (bf16[16,128,512]{2,1,0:T(8,128)(2,1)S(1)}, bf16[16,128,512]{2,1,0:T(8,128)(2,1)}, u32[]{:S(2)}) copy-start(bf16[16,128,512]{2,1,0:T(8,128)(2,1)} %param.7) | copy-start | bytes 6291460
  8.0 15.6 %all-to-all-start = ((s32[8,128,2]{1,2,0:T(2,128)}), s32[8,128,2]{1,2,0:T(2,128)S(1)}, u32[]{:S(2)}, u32[]{:S(2)}) async-start(s32[8,128,2]{1,2,0:T(2,128)} %broadcast_in_dim.17), calls=%async_computation | async-start | bytes 16384 | tf_op jit(solution)/shard_map/all_to_all | solution.py:13
  15.9 369.4 %reduce-scatter.2.cloned.1.call-start = ((), (), s32[]{:S(2)}) async-start(), calls=%async_computation.5 | async-start | bytes 15597568 | tf_op jit(solution)/shard_map/reduce_scatter | solution.py:95
  55.6 190.4 %slice-start = ((s8[7340032]{0:T(1024)(128)(4,1)}), s8[4194304]{0:T(1024)(128)(4,1)S(1)}, s32[]{:S(2)}) async-start(s8[7340032]{0:T(1024)(128)(4,1)} %bitcast.99), calls=%async_computation.6 | async-start | bytes 8388608
  224.2 21.8 %slice-start.1 = ((s8[7340032]{0:T(1024)(128)(4,1)}), s8[3145728]{0:T(1024)(128)(4,1)S(1)}, s32[]{:S(2)}) async-start(s8[7340032]{0:T(1024)(128)(4,1)} %bitcast.99), calls=%async_computation.7 | async-start | bytes 6291456
  301.3 93.5 %copy-start.2 = (f32[128]{0:T(128)S(1)}, f32[128]{0:T(128)}, u32[]{:S(2)}) copy-start(f32[128]{0:T(128)} %param.11) | copy-start | bytes 1540
  301.3 110.8 %copy-start.1 = (bf16[16,128,512]{2,1,0:T(8,128)(2,1)S(1)}, bf16[16,128,512]{2,1,0:T(8,128)(2,1)}, u32[]{:S(2)}) copy-start(bf16[16,128,512]{2,1,0:T(8,128)(2,1)} %param.7) | copy-start | bytes 6291460
  387.7 20.6 %all-to-all-start.3 = ((bf16[8,1,14,4096]{3,2,1,0:T(8,128)(2,1)}), bf16[8,1,14,4096]{3,2,1,0:T(8,128)(2,1)S(1)}, u32[]{:S(2)}, u32[]{:S(2)}) async-start(bf16[8,1,14,4096]{3,2,1,0:T(8,128)(2,1)} %bitcast.90), calls=%async_computation.4 | async-start | bytes 2097152 | tf_op jit(solution)/shard_map/all_to_all | solution.py:102
Sparse Core Ops, SparseCore 0:
  301.4 83.7 reduce-scatter.1
